TPU v7x, 32 devices: a whole 2x2x4 slice. The times are simulated.
32 devices in a mesh: mem: 2 (over x), col: 16 (over z, y, core).
Axes of the slice: x: 2, y: 2, z: 4, core: 2. Of those that a mesh axis runs over, the one named last changes fastest.
Arguments:
- state_a: bfloat16 [64, 1048576], P('mem', 'col'), may hold values from -12 to 12
- state_b: bfloat16 [64, 1048576], P('mem', 'col'), may hold values from -12 to 12
- obs_index: int32 [2, 8192, 16], P(None, ('col', 'mem')), may hold values from 0 to 127
- observation_count: int32 [2, 8192], P(None, ('col', 'mem')), may hold values from 1 to 16, as said below
- obs_value: float32 [2, 8192, 16], P(None, ('col', 'mem')), may hold values from -32 to 32
- obs_weight: float32 [2, 8192, 16], P(None, ('col', 'mem')), may hold values from 0.02 to 0.2
Outputs:
- analysis_a: bfloat16 [64, 1048576], P(None, ('col', 'mem'))
- analysis_b: bfloat16 [64, 1048576], P(None, ('col', 'mem'))
- transform: float32 [64, 64], replicated
Inputs may be any that keep to these rules, and one draw needn't show every extreme that they name: Slot s of block b of group g is an observation when s < observation_count[g, b]; for each group, every aligned run of 256 blocks holds a block with all 16 slots live.
All inputs are finite; a program needn't handle non-finite values.
Results may differ from a plain program's by a relative error of at most 0.005.
Values may be sent and summed in bfloat16 or wider, within the bound.
A program may use at most 64 MiB of HBM per device.

v0:
```python
import jax
import jax.numpy as jnp
from jax import lax
from jax.sharding import PartitionSpec as P

ITERS = 24


def inverse_root(amat):
    scale = jnp.sqrt(jnp.sum(amat * amat))
    eye = jnp.eye(amat.shape[0], dtype=jnp.float32)

    def forward_step(step, carry):
        yn, zn = carry
        tm = 1.5 * eye - 0.5 * jnp.dot(zn, yn, precision=lax.Precision.HIGHEST)
        return (
            jnp.dot(yn, tm, precision=lax.Precision.HIGHEST),
            jnp.dot(tm, zn, precision=lax.Precision.HIGHEST),
        )

    yn, zn = lax.fori_loop(0, ITERS, forward_step, (amat / scale, eye))
    return (zn, scale)


def make_transform(gram_product, cross, misfit, total):
    members = gram_product.shape[0]
    scl = (members - 1.0) / total
    gs = scl * gram_product
    bs = scl * cross
    qval = scl * misfit
    tval = jnp.trace(gs)
    rho = (1.0 + qval / (members - 1.0)) / (1.0 + tval / (members - 1.0))
    amat = (members - 1.0) / rho * jnp.eye(members, dtype=jnp.float32) + gs
    zn, scale = inverse_root(amat)
    pmat = jnp.dot(zn, zn, precision=lax.Precision.HIGHEST) / scale
    wbar = jnp.dot(pmat, bs, precision=lax.Precision.HIGHEST)
    return jnp.sqrt(members - 1.0) * zn / jnp.sqrt(scale) + wbar[:, None]


def shards(state_a, state_b, obs_index, observation_count, obs_value, obs_weight):
    members = state_a.shape[0]
    group_column_sets = state_a.shape[1]
    nmem = lax.axis_size("mem")
    piece = group_column_sets // nmem
    everyone = members * nmem
    nblk = obs_index.shape[1]
    slots = obs_index.shape[2]
    width = nblk * slots
    live = (
        lax.broadcasted_iota(jnp.int32, (2, nblk, slots), 2) < observation_count[:, :, None]
    ).astype(jnp.float32)
    live = live.reshape(2, width)
    weights = live * obs_weight.reshape(2, width)
    observed = obs_value.reshape(2, width)

    def observe(columns, index, blocks):
        lanes = lax.broadcasted_iota(jnp.int32, (blocks, slots, 128), 2)
        onehot = (index[:, :, None] == lanes).astype(jnp.bfloat16)
        taken = jnp.einsum(
            "kbc,bsc->kbs",
            columns.reshape(columns.shape[0], blocks, 128),
            onehot,
            preferred_element_type=jnp.float32,
        )
        return taken.reshape(columns.shape[0], blocks * slots)

    def statistics(hx, group):
        hmean = jnp.mean(hx, axis=0)
        anomaly_rows = hx - hmean[None]
        innov = observed[group] - hmean
        wt = weights[group]
        scaled_anomaly = anomaly_rows * wt[None]
        gram_product = jnp.einsum(
            "kn,ln->kl", scaled_anomaly, anomaly_rows, precision=lax.Precision.HIGHEST
        )
        cross = jnp.einsum("kn,n->k", scaled_anomaly, innov, precision=lax.Precision.HIGHEST)
        misfit = jnp.sum(wt * innov * innov)
        extra = jnp.stack([misfit, jnp.sum(live[group])])
        return (gram_product, cross, extra)

    def regroup(state):
        return state.reshape(members, nmem, piece)

    all_index = lax.all_gather(obs_index, "mem", axis=1, tiled=True)
    local_hx = jnp.stack(
        [observe(state_a, all_index[0], nmem * nblk), observe(state_b, all_index[1], nmem * nblk)]
    ).astype(jnp.bfloat16)
    moved_hx = lax.all_to_all(
        local_hx.reshape(2, members, nmem, width), "mem", split_axis=2, concat_axis=1, tiled=True
    )
    hx_all = moved_hx.reshape(2, everyone, width).astype(jnp.float32)
    first = statistics(hx_all[0], 0)
    second = statistics(hx_all[1], 1)
    gram_product, cross, extra = lax.psum(
        (first[0] + second[0], first[1] + second[1], first[2] + second[2]), ("mem", "col")
    )
    moved_a, moved_b = (
        lax.all_to_all(regroup(state_a), "mem", split_axis=1, concat_axis=0, tiled=True),
        lax.all_to_all(regroup(state_b), "mem", split_axis=1, concat_axis=0, tiled=True),
    )
    columns = [moved_a.reshape(everyone, piece), moved_b.reshape(everyone, piece)]
    misfit = extra[0]
    total = extra[1]
    transform = make_transform(gram_product, cross, misfit, total)
    wb = transform.astype(jnp.bfloat16)
    column_total = jnp.sum(wb.astype(jnp.float32), axis=0)
    ones = jnp.ones((everyone,), jnp.bfloat16)

    def analyse(cols):
        xmean = jnp.dot(ones, cols, preferred_element_type=jnp.float32) / everyone
        mixed = jnp.dot(wb.T, cols, preferred_element_type=jnp.float32)
        return (mixed + xmean[None, :] * (1.0 - column_total)[:, None]).astype(jnp.bfloat16)

    return (analyse(columns[0]), analyse(columns[1]), transform)


def solution(mesh):
    return jax.shard_map(
        shards,
        mesh=mesh,
        in_specs=(
            P("mem", "col"),
            P("mem", "col"),
            P(None, ("col", "mem"), None),
            P(None, ("col", "mem")),
            P(None, ("col", "mem"), None),
            P(None, ("col", "mem"), None),
        ),
        out_specs=(P(None, ("col", "mem")), P(None, ("col", "mem")), P()),
        check_vma=False,
    )
```

profile of v0, /device:TPU:0, one launch (start us, length us, event | category | flops | bytes accessed | tf_op | source)
XLA Modules:
  0.0 192.1 jit_solution(10022677384199641888)
XLA Ops:
  0.6 5.8 %all_gather.3 = s32[2,512,16]{1,2,0:T(8,128)S(1)} all-gather(s32[2,256,16]{1,2,0:T(8,128)} %param.10), channel_id=1, replica_groups=mesh['mem'=2,'col'=16] {'mem'}, dimensions={1}, use_global_device_ids=true | all-gather | bytes 98304 | tf_op jit(solution)/shard_map/all_gather | solution.py:84
  6.7 4.6 %fusion.16 = bf16[512,16,32]{2,1,0:T(8,128)(2,1)S(1)} fusion(s32[512,16]{1,0:T(8,128)S(1)} %copy.40, bf16[32,65536]{1,0:T(8,128)(2,1)} %param.9), kind=kOutput, calls=%fused_computation.23 | convolution fusion | flops 68419584 | bytes 4751360 | tf_op jit(solution)/shard_map/kbc,bsc->kbs/dot_general | solution.py:59
  11.3 0.8 copy.43
  12.1 4.6 %fusion.13 = bf16[512,16,32]{2,1,0:T(8,128)(2,1)S(1)} fusion(s32[512,16]{1,0:T(8,128)S(1)} %copy.38, bf16[32,65536]{1,0:T(8,128)(2,1)} %param.8), kind=kOutput, calls=%fused_computation.22 | convolution fusion | flops 68419584 | bytes 4751360 | tf_op jit(solution)/shard_map/kbc,bsc->kbs/dot_general | solution.py:59
  16.7 0.8 copy.42
  17.5 1.1 pad_maximum_fusion
  18.6 3.6 %all-to-all-start = ((bf16[2,32,2,4096]{3,1,0,2:T(8,128)(2,1)}), bf16[2,32,2,4096]{3,1,0,2:T(8,128)(2,1)S(1)}, u32[]{:S(2)}, u32[]{:S(2)}) async-start(bf16[2,32,2,4096]{3,1,0,2:T(8,128)(2,1)} %pad_maximum_fusion), calls=%async_computation | async-start | bytes 2097152 | tf_op jit(solution)/shard_map/all_to_all | solution.py:88
  23.2 0.7 slice_reduce_fusion
  24.2 4.6 %copy.70 = bf16[4,2,8,32768]{3,2,0,1:T(8,128)(2,1)} copy(bf16[4,2,8,32768]{3,2,1,0:T(8,128)(2,1)} %bitcast.125) | data formatting | bytes 8388608 | tf_op jit(solution)/shard_map/reshape | solution.py:82
  28.8 2.3 %copy.71 = bf16[4,2,8,32768]{3,2,0,1:T(8,128)(2,1)} copy(bf16[4,2,8,32768]{3,2,1,0:T(8,128)(2,1)S(1)} %bitcast.126) | data formatting | bytes 8388608 | tf_op jit(solution)/shard_map/reshape | solution.py:82
  31.2 4.0 %all-to-all-done = bf16[2,32,2,4096]{3,1,0,2:T(8,128)(2,1)S(1)} async-done(((bf16[2,32,2,4096]{3,1,0,2:T(8,128)(2,1)}), bf16[2,32,2,4096]{3,1,0,2:T(8,128)(2,1)S(1)}, u32[]{:S(2)}, u32[]{:S(2)}) %all-to-all-start) | async-done | bytes 1048608 | tf_op jit(solution)/shard_map/all_to_all | solution.py:88
  35.1 5.6 %all-to-all-start.2 = ((bf16[32,2,32768]{2,0,1:T(8,128)(2,1)}), bf16[32,2,32768]{2,0,1:T(8,128)(2,1)}, u32[]{:S(2)}, u32[]{:S(2)}) async-start(bf16[32,2,32768]{2,0,1:T(8,128)(2,1)} %bitcast.124), calls=%async_computation.2 | async-start | bytes 8388608 | tf_op jit(solution)/shard_map/all_to_all | solution.py:99
  40.8 0.2 convert_bitcast_fusion
  41.0 0.3 slice_reduce_fusion.2
  41.3 0.6 fusion.38
  42.1 0.7 fusion.39
  43.0 2.6 %maximum_add_fusion = f32[2]{0:T(128)S(1)} fusion(f32[1]{0:T(128)} %bitcast.10, f32[1]{0:T(128)} %bitcast.9, f32[1]{0:T(128)} %bitcast.14, f32[1]{0:T(128)} %bitcast.13), kind=kLoop, calls=%fused_computation.71 | loop fusion | flops 6 | bytes 24 | tf_op jit(solution)/shard_map/add | solution.py:95
  45.6 0.2 bitcast_subtract_fusion
  45.8 0.9 convolution_bitcast_fusion.1
  46.7 1.0 fusion.19
  47.7 1.0 fusion.25
  48.7 1.0 convolution_add_fusion.2
  49.7 71.5 %all-reduce = (f32[64,64]{1,0:T(8,128)S(1)}, f32[2]{0:T(128)S(1)}, f32[64]{0:T(128)S(1)}) all-reduce(f32[64,64]{1,0:T(8,128)S(1)} %convolution_add_fusion.2, f32[2]{0:T(128)S(1)} %maximum_add_fusion, f32[64]{0:T(128)S(1)} %fusion.19), channel_id=1, replica_groups=mesh['mem'=2,'col'=16] {'mem','col'}, use_global_device_ids=true, to_apply=%region_7.0 | all-reduce | flops 4162 | bytes 33296 | tf_op jit(solution)/shard_map/psum | solution.py:94
  121.2 0.6 fusion.53
  123.1 0.6 select_reduce_fusion
  124.4 0.6 multiply_reduce_fusion
  125.8 5.8 %all-to-all-start.1 = ((bf16[32,2,32768]{2,0,1:T(8,128)(2,1)}), bf16[32,2,32768]{2,0,1:T(8,128)(2,1)}, u32[]{:S(2)}, u32[]{:S(2)}) async-start(bf16[32,2,32768]{2,0,1:T(8,128)(2,1)} %bitcast.123), calls=%async_computation.1 | async-start | bytes 8388608 | tf_op jit(solution)/shard_map/all_to_all | solution.py:98
  131.6 15.5 %while.13 = (s32[]{:T(128)}, f32[64,64]{0,1:T(8,128)S(1)}, f32[64,64]{1,0:T(8,128)S(1)}, s32[]{:T(128)}) while((s32[]{:T(128)}, f32[64,64]{0,1:T(8,128)S(1)}, f32[64,64]{1,0:T(8,128)S(1)}, s32[]{:T(128)}) %tuple.41), condition=%wide.region_11.12_spmd.clone, body=%wide.region_10.11_spmd.clone.sunk | while | flops 9453570 | bytes 213045 | solution.py:21
  131.6 0.2 fusion.86
  132.0 0.2 convolution_bitcast_fusion.5
  132.6 0.2 convolution_bitcast_fusion.5
  132.9 0.2 fusion.86
  133.3 0.2 convolution_bitcast_fusion.5
  133.9 0.2 convolution_bitcast_fusion.5
  134.2 0.2 fusion.86
  134.5 0.2 convolution_bitcast_fusion.5
  135.2 0.2 convolution_bitcast_fusion.5
  135.5 0.2 fusion.86
  135.8 0.2 convolution_bitcast_fusion.5
  136.5 0.2 convolution_bitcast_fusion.5
  136.8 0.2 fusion.86
  137.1 0.2 convolution_bitcast_fusion.5
  137.8 0.2 convolution_bitcast_fusion.5
  138.0 0.2 fusion.86
  138.4 0.2 convolution_bitcast_fusion.5
  139.0 0.2 convolution_bitcast_fusion.5
  139.3 0.2 fusion.86
  139.7 0.2 convolution_bitcast_fusion.5
  140.3 0.2 convolution_bitcast_fusion.5
  141.0 0.2 convolution_bitcast_fusion.5
  141.6 0.2 convolution_bitcast_fusion.5
  142.3 0.2 convolution_bitcast_fusion.5
  142.9 0.2 convolution_bitcast_fusion.5
  143.6 0.2 convolution_bitcast_fusion.5
  144.2 0.2 convolution_bitcast_fusion.5
  144.8 0.2 convolution_bitcast_fusion.5
  145.5 0.2 convolution_bitcast_fusion.5
  146.1 0.2 convolution_bitcast_fusion.5
  146.8 0.2 convolution_bitcast_fusion.5
  147.5 2.8 %fusion.42 = f32[1,32768]{1,0:T(1,128)S(1)} fusion(bf16[64,32768]{1,0:T(8,128)(2,1)} %bitcast.35), kind=kOutput, calls=%fused_computation.74 | convolution fusion | flops 4194304 | bytes 4325376 | tf_op jit(solution)/shard_map/dot_general | solution.py:110
  150.4 27.9 %all-to-all-done.1 = bf16[32,2,32768]{2,0,1:T(8,128)(2,1)} async-done(((bf16[32,2,32768]{2,0,1:T(8,128)(2,1)}), bf16[32,2,32768]{2,0,1:T(8,128)(2,1)}, u32[]{:S(2)}, u32[]{:S(2)}) %all-to-all-start.1) | async-done | bytes 4194336 | tf_op jit(solution)/shard_map/all_to_all | solution.py:98
  178.3 2.8 %fusion.44 = f32[1,32768]{1,0:T(1,128)S(1)} fusion(bf16[64,32768]{1,0:T(8,128)(2,1)} %bitcast.29), kind=kOutput, calls=%fused_computation.76 | convolution fusion | flops 4194304 | bytes 4325376 | tf_op jit(solution)/shard_map/dot_general | solution.py:110
  181.1 5.5 %fusion.4 = bf16[64,32768]{1,0:T(8,128)(2,1)} fusion(bf16[64,32768]{1,0:T(8,128)(2,1)} %bitcast.35, f32[32768]{0:T(1024)S(1)} %broadcast_multiply_fusion, f32[64]{0:T(128)S(1)} %broadcast_subtract_fusion, f32[64,64]{1,0:T(8,128)S(1)} %get-tuple-element.60), kind=kOutput, calls=%fused_computation.8 | convolution fusion | flops 274731008 | bytes 8536320 | tf_op jit(solution)/shard_map/dot_general | solution.py:111
  186.6 5.5 %fusion.3 = bf16[64,32768]{1,0:T(8,128)(2,1)} fusion(bf16[64,32768]{1,0:T(8,128)(2,1)} %bitcast.29, f32[64]{0:T(128)S(1)} %broadcast_subtract_fusion, f32[32768]{0:T(1024)S(1)} %broadcast_multiply_fusion.1, f32[64,64]{1,0:T(8,128)S(1)} %get-tuple-element.60), kind=kOutput, calls=%fused_computation.7 | convolution fusion | flops 274731008 | bytes 8536320 | tf_op jit(solution)/shard_map/dot_general | solution.py:111
  (132 shorter events, 9.8 us)
Async XLA Ops:
  16.6 5.5 %copy-start.3 = (f32[2,256,16]{1,2,0:T(8,128)S(1)}, f32[2,256,16]{1,2,0:T(8,128)}, u32[]{:S(2)}) copy-start(f32[2,256,16]{1,2,0:T(8,128)} %param.12) | copy-start | bytes 98308
  16.7 6.1 %copy-start.2 = (f32[2,256,16]{1,2,0:T(8,128)S(1)}, f32[2,256,16]{1,2,0:T(8,128)}, u32[]{:S(2)}) copy-start(f32[2,256,16]{1,2,0:T(8,128)} %param.13) | copy-start | bytes 98308
  16.7 6.4 %copy-start.4 = (s32[2,256]{1,0:T(2,128)S(1)}, s32[2,256]{1,0:T(2,128)}, u32[]{:S(2)}) copy-start(s32[2,256]{1,0:T(2,128)} %param.11) | copy-start | bytes 6148
  18.6 16.6 %all-to-all-start = ((bf16[2,32,2,4096]{3,1,0,2:T(8,128)(2,1)}), bf16[2,32,2,4096]{3,1,0,2:T(8,128)(2,1)S(1)}, u32[]{:S(2)}, u32[]{:S(2)}) async-start(bf16[2,32,2,4096]{3,1,0,2:T(8,128)(2,1)} %pad_maximum_fusion), calls=%async_computation | async-start | bytes 2097152 | tf_op jit(solution)/shard_map/all_to_all | solution.py:88
  24.1 4.6 %copy-start = (bf16[32,65536]{1,0:T(8,128)(2,1)S(1)}, bf16[32,65536]{1,0:T(8,128)(2,1)}, u32[]{:S(2)}) copy-start(bf16[32,65536]{1,0:T(8,128)(2,1)} %param.8) | copy-start | bytes 12582916
  35.1 90.6 %all-to-all-start.2 = ((bf16[32,2,32768]{2,0,1:T(8,128)(2,1)}), bf16[32,2,32768]{2,0,1:T(8,128)(2,1)}, u32[]{:S(2)}, u32[]{:S(2)}) async-start(bf16[32,2,32768]{2,0,1:T(8,128)(2,1)} %bitcast.124), calls=%async_computation.2 | async-start | bytes 8388608 | tf_op jit(solution)/shard_map/all_to_all | solution.py:99
  125.8 52.5 %all-to-all-start.1 = ((bf16[32,2,32768]{2,0,1:T(8,128)(2,1)}), bf16[32,2,32768]{2,0,1:T(8,128)(2,1)}, u32[]{:S(2)}, u32[]{:S(2)}) async-start(bf16[32,2,32768]{2,0,1:T(8,128)(2,1)} %bitcast.123), calls=%async_computation.1 | async-start | bytes 8388608 | tf_op jit(solution)/shard_map/all_to_all | solution.py:98
  147.5 39.1 %copy-start.1 = (f32[64,64]{1,0:T(8,128)}, f32[64,64]{1,0:T(8,128)S(1)}, u32[]{:S(2)}) copy-start(f32[64,64]{1,0:T(8,128)S(1)} %get-tuple-element.60) | copy-start | bytes 49156
where the time goes:
time: 193 us; the launch traced here: 192 us
  blocking collectives  77.2 us (40%)
  matrix products  44 us (23%)
  waiting for transfers between devices  31.8 us (16%)
  starting transfers between devices  15 us (8%)
  local copies, waits for them, and re-layouts  11.2 us (6%)
  other arithmetic  7.89 us (4%)
  between operations  3.67 us (2%)
    psum x1, blocking collectives, shards(): lax.psum((first[0] + second[0], first[1] + second[1], first[2] + second[2...  71.5 us
    all_to_all x1, waiting for transfers between devices, shards(): lax.all_to_all(regroup(state_a), 'mem', split_axis=1, concat_axis=0, tile...  27.9 us
    dot_general x2, matrix products, analyse(): mixed = jnp.dot(wb.T, cols, preferred_element_type=jnp.float32)  11 us
    dot_general x2, matrix products, observe(): jnp.einsum('kbc,bsc->kbs', columns.reshape(columns.shape[0], blocks, 128)...  9.13 us
    reshape x2, local copies, waits for them, and re-layouts, regroup(): return state.reshape(members, nmem, piece)  6.94 us
    all_gather x1, blocking collectives, shards(): all_index = lax.all_gather(obs_index, 'mem', axis=1, tiled=True)  5.79 us
    all_to_all x1, starting transfers between devices, shards(): lax.all_to_all(regroup(state_a), 'mem', split_axis=1, concat_axis=0, tile...  5.79 us
    dot_general x2, matrix products, analyse(): xmean = jnp.dot(ones, cols, preferred_element_type=jnp.float32) / everyone  5.68 us
  transfers between devices with their start and end apart: 3, of which 2 were waited for; matrix products, arithmetic and copies ran while one was open for 19% of the time, Pallas kernels for 0%

commit v1 on v0

--- a/solution.py
+++ b/solution.py
@@ -92,7 +92,7 @@
     first = statistics(hx_all[0], 0)
     second = statistics(hx_all[1], 1)
     gram_product, cross, extra = lax.psum(
-        (first[0] + second[0], first[1] + second[1], first[2] + second[2]), ("mem", "col")
+        lax.psum((first[0] + second[0], first[1] + second[1], first[2] + second[2]), "mem"), "col"
     )
     moved_a, moved_b = (
         lax.all_to_all(regroup(state_a), "mem", split_axis=1, concat_axis=0, tiled=True),

time: 193 us -> 216 us (1.12)
  blocking collectives: 77.2 us -> 104 us
  waiting for transfers between devices: 31.8 us -> 28.3 us
    psum x0 -> x1, blocking collectives: none -> 58.6 us  [shards(): lax.psum(lax.psum((first[0] + second[0], first[1] + second[1], first[2] +...]
    psum x1, blocking collectives: 71.5 us -> 39.4 us  [shards(): lax.psum((first[0] + second[0], first[1] + second[1], first[2] + second[2...]
    all_to_all x1, waiting for transfers between devices: 27.9 us -> 24.3 us  [shards(): lax.all_to_all(regroup(state_a), 'mem', split_axis=1, concat_axis=0, tile...]
  transfers between devices with their start and end apart: 3 -> 3, of which waited for: 2 -> 2; matrix products, arithmetic and copies ran while one was open for 19% -> 17% of each run, Pallas kernels for 0% -> 0%
where the time goes in v1:
time: 216 us; the launch traced here: 215 us
  blocking collectives  104 us (48%)
  matrix products  44 us (20%)
  waiting for transfers between devices  28.3 us (13%)
  starting transfers between devices  15 us (7%)
  local copies, waits for them, and re-layouts  11.2 us (5%)
  other arithmetic  7.9 us (4%)
  between operations  3.67 us (2%)
    psum x1, blocking collectives, shards(): lax.psum(lax.psum((first[0] + second[0], first[1] + second[1], first[2] +...  58.6 us
    psum x1, blocking collectives, shards(): lax.psum((first[0] + second[0], first[1] + second[1], first[2] + second[2...  39.4 us
    all_to_all x1, waiting for transfers between devices, shards(): lax.all_to_all(regroup(state_a), 'mem', split_axis=1, concat_axis=0, tile...  24.3 us
    dot_general x2, matrix products, analyse(): mixed = jnp.dot(wb.T, cols, preferred_element_type=jnp.float32)  11 us
    dot_general x2, matrix products, observe(): jnp.einsum('kbc,bsc->kbs', columns.reshape(columns.shape[0], blocks, 128)...  9.13 us
    reshape x2, local copies, waits for them, and re-layouts, regroup(): return state.reshape(members, nmem, piece)  6.94 us
    all_gather x1, blocking collectives, shards(): all_index = lax.all_gather(obs_index, 'mem', axis=1, tiled=True)  5.79 us
    all_to_all x1, starting transfers between devices, shards(): lax.all_to_all(regroup(state_a), 'mem', split_axis=1, concat_axis=0, tile...  5.79 us
  transfers between devices with their start and end apart: 3, of which 2 were waited for; matrix products, arithmetic and copies ran while one was open for 17% of the time, Pallas kernels for 0%

profile of v1, /device:TPU:0, one launch (start us, length us, event | category | flops | bytes accessed | tf_op | source)
XLA Modules:
  0.0 215.1 jit_solution(15622349304442020659)
XLA Ops:
  0.6 5.8 %all_gather.3 = s32[2,512,16]{1,2,0:T(8,128)S(1)} all-gather(s32[2,256,16]{1,2,0:T(8,128)} %param.10), channel_id=1, replica_groups=mesh['mem'=2,'col'=16] {'mem'}, dimensions={1}, use_global_device_ids=true | all-gather | bytes 98304 | tf_op jit(solution)/shard_map/all_gather | solution.py:84
  6.7 4.6 %fusion.16 = bf16[512,16,32]{2,1,0:T(8,128)(2,1)S(1)} fusion(s32[512,16]{1,0:T(8,128)S(1)} %copy.40, bf16[32,65536]{1,0:T(8,128)(2,1)} %param.9), kind=kOutput, calls=%fused_computation.23 | convolution fusion | flops 68419584 | bytes 4751360 | tf_op jit(solution)/shard_map/kbc,bsc->kbs/dot_general | solution.py:59
  11.3 0.8 copy.43
  12.1 4.6 %fusion.13 = bf16[512,16,32]{2,1,0:T(8,128)(2,1)S(1)} fusion(s32[512,16]{1,0:T(8,128)S(1)} %copy.38, bf16[32,65536]{1,0:T(8,128)(2,1)} %param.8), kind=kOutput, calls=%fused_computation.22 | convolution fusion | flops 68419584 | bytes 4751360 | tf_op jit(solution)/shard_map/kbc,bsc->kbs/dot_general | solution.py:59
  16.7 0.8 copy.42
  17.5 1.1 pad_maximum_fusion
  18.6 3.6 %all-to-all-start = ((bf16[2,32,2,4096]{3,1,0,2:T(8,128)(2,1)}), bf16[2,32,2,4096]{3,1,0,2:T(8,128)(2,1)S(1)}, u32[]{:S(2)}, u32[]{:S(2)}) async-start(bf16[2,32,2,4096]{3,1,0,2:T(8,128)(2,1)} %pad_maximum_fusion), calls=%async_computation | async-start | bytes 2097152 | tf_op jit(solution)/shard_map/all_to_all | solution.py:88
  23.2 0.7 slice_reduce_fusion
  24.2 4.6 %copy.70 = bf16[4,2,8,32768]{3,2,0,1:T(8,128)(2,1)} copy(bf16[4,2,8,32768]{3,2,1,0:T(8,128)(2,1)} %bitcast.125) | data formatting | bytes 8388608 | tf_op jit(solution)/shard_map/reshape | solution.py:82
  28.8 2.3 %copy.71 = bf16[4,2,8,32768]{3,2,0,1:T(8,128)(2,1)} copy(bf16[4,2,8,32768]{3,2,1,0:T(8,128)(2,1)S(1)} %bitcast.126) | data formatting | bytes 8388608 | tf_op jit(solution)/shard_map/reshape | solution.py:82
  31.2 4.0 %all-to-all-done = bf16[2,32,2,4096]{3,1,0,2:T(8,128)(2,1)S(1)} async-done(((bf16[2,32,2,4096]{3,1,0,2:T(8,128)(2,1)}), bf16[2,32,2,4096]{3,1,0,2:T(8,128)(2,1)S(1)}, u32[]{:S(2)}, u32[]{:S(2)}) %all-to-all-start) | async-done | bytes 1048608 | tf_op jit(solution)/shard_map/all_to_all | solution.py:88
  35.1 5.6 %all-to-all-start.2 = ((bf16[32,2,32768]{2,0,1:T(8,128)(2,1)}), bf16[32,2,32768]{2,0,1:T(8,128)(2,1)}, u32[]{:S(2)}, u32[]{:S(2)}) async-start(bf16[32,2,32768]{2,0,1:T(8,128)(2,1)} %bitcast.124), calls=%async_computation.2 | async-start | bytes 8388608 | tf_op jit(solution)/shard_map/all_to_all | solution.py:99
  40.8 0.2 convert_bitcast_fusion
  41.0 0.3 slice_reduce_fusion.2
  41.2 0.7 fusion.39
  41.9 0.6 fusion.38
  42.5 0.3 bitcast_subtract_fusion
  43.3 2.6 %maximum_add_fusion = f32[2]{0:T(128)S(1)} fusion(f32[1]{0:T(128)} %bitcast.10, f32[1]{0:T(128)} %bitcast.9, f32[1]{0:T(128)} %bitcast.14, f32[1]{0:T(128)} %bitcast.13), kind=kLoop, calls=%fused_computation.71 | loop fusion | flops 6 | bytes 24 | tf_op jit(solution)/shard_map/add | solution.py:95
  45.8 0.9 convolution_bitcast_fusion.1
  46.7 1.0 fusion.19
  47.7 1.0 fusion.25
  48.7 1.0 convolution_add_fusion.2
  49.8 39.4 %all-reduce.1 = (f32[64,64]{1,0:T(8,128)S(1)}, f32[2]{0:T(128)S(1)}, f32[64]{0:T(128)S(1)}) all-reduce(f32[64,64]{1,0:T(8,128)S(1)} %convolution_add_fusion.2, f32[2]{0:T(128)S(1)} %maximum_add_fusion, f32[64]{0:T(128)S(1)} %fusion.19), channel_id=1, replica_groups=mesh['mem'=2,'col'=16] {'mem'}, use_global_device_ids=true, to_apply=%region_8.0 | all-reduce | flops 4162 | bytes 33296 | tf_op jit(solution)/shard_map/psum | solution.py:95
  89.2 58.6 %all-reduce = (f32[64,64]{1,0:T(8,128)S(1)}, f32[2]{0:T(128)S(1)}, f32[64]{0:T(128)S(1)}) all-reduce(f32[64,64]{1,0:T(8,128)S(1)} %get-tuple-element.59, f32[2]{0:T(128)S(1)} %get-tuple-element.60, f32[64]{0:T(128)S(1)} %get-tuple-element.61), channel_id=1, replica_groups=mesh['mem'=2,'col'=16] {'col'}, use_global_device_ids=true, to_apply=%region_9.0 | all-reduce | flops 4162 | bytes 33296 | tf_op jit(solution)/shard_map/psum | solution.py:94
  147.8 0.6 fusion.53
  149.6 0.6 select_reduce_fusion
  150.9 0.6 multiply_reduce_fusion
  152.3 5.8 %all-to-all-start.1 = ((bf16[32,2,32768]{2,0,1:T(8,128)(2,1)}), bf16[32,2,32768]{2,0,1:T(8,128)(2,1)}, u32[]{:S(2)}, u32[]{:S(2)}) async-start(bf16[32,2,32768]{2,0,1:T(8,128)(2,1)} %bitcast.123), calls=%async_computation.1 | async-start | bytes 8388608 | tf_op jit(solution)/shard_map/all_to_all | solution.py:98
  158.1 15.5 %while.13 = (s32[]{:T(128)}, f32[64,64]{0,1:T(8,128)S(1)}, f32[64,64]{1,0:T(8,128)S(1)}, s32[]{:T(128)}) while((s32[]{:T(128)}, f32[64,64]{0,1:T(8,128)S(1)}, f32[64,64]{1,0:T(8,128)S(1)}, s32[]{:T(128)}) %tuple.41), condition=%wide.region_13.14_spmd.clone, body=%wide.region_12.13_spmd.clone.sunk | while | flops 9453570 | bytes 213045 | solution.py:21
  158.2 0.2 fusion.86
  158.5 0.2 convolution_bitcast_fusion.5
  159.2 0.2 convolution_bitcast_fusion.5
  159.4 0.2 fusion.86
  159.8 0.2 convolution_bitcast_fusion.5
  160.5 0.2 convolution_bitcast_fusion.5
  160.7 0.2 fusion.86
  161.1 0.2 convolution_bitcast_fusion.5
  161.7 0.2 convolution_bitcast_fusion.5
  162.0 0.2 fusion.86
  162.4 0.2 convolution_bitcast_fusion.5
  163.0 0.2 convolution_bitcast_fusion.5
  163.3 0.2 fusion.86
  163.7 0.2 convolution_bitcast_fusion.5
  164.3 0.2 convolution_bitcast_fusion.5
  164.6 0.2 fusion.86
  165.0 0.2 convolution_bitcast_fusion.5
  165.6 0.2 convolution_bitcast_fusion.5
  166.3 0.2 convolution_bitcast_fusion.5
  166.9 0.2 convolution_bitcast_fusion.5
  167.5 0.2 convolution_bitcast_fusion.5
  168.2 0.2 convolution_bitcast_fusion.5
  168.8 0.2 convolution_bitcast_fusion.5
  169.5 0.2 convolution_bitcast_fusion.5
  170.1 0.2 convolution_bitcast_fusion.5
  170.8 0.2 convolution_bitcast_fusion.5
  171.4 0.2 convolution_bitcast_fusion.5
  172.1 0.2 convolution_bitcast_fusion.5
  172.7 0.2 convolution_bitcast_fusion.5
  173.3 0.2 convolution_bitcast_fusion.5
  174.1 2.8 %fusion.42 = f32[1,32768]{1,0:T(1,128)S(1)} fusion(bf16[64,32768]{1,0:T(8,128)(2,1)} %bitcast.35), kind=kOutput, calls=%fused_computation.74 | convolution fusion | flops 4194304 | bytes 4325376 | tf_op jit(solution)/shard_map/dot_general | solution.py:110
  177.0 24.3 %all-to-all-done.1 = bf16[32,2,32768]{2,0,1:T(8,128)(2,1)} async-done(((bf16[32,2,32768]{2,0,1:T(8,128)(2,1)}), bf16[32,2,32768]{2,0,1:T(8,128)(2,1)}, u32[]{:S(2)}, u32[]{:S(2)}) %all-to-all-start.1) | async-done | bytes 4194336 | tf_op jit(solution)/shard_map/all_to_all | solution.py:98
  201.3 2.8 %fusion.44 = f32[1,32768]{1,0:T(1,128)S(1)} fusion(bf16[64,32768]{1,0:T(8,128)(2,1)} %bitcast.29), kind=kOutput, calls=%fused_computation.76 | convolution fusion | flops 4194304 | bytes 4325376 | tf_op jit(solution)/shard_map/dot_general | solution.py:110
  204.1 5.5 %fusion.4 = bf16[64,32768]{1,0:T(8,128)(2,1)} fusion(bf16[64,32768]{1,0:T(8,128)(2,1)} %bitcast.35, f32[32768]{0:T(1024)S(1)} %broadcast_multiply_fusion, f32[64]{0:T(128)S(1)} %broadcast_subtract_fusion, f32[64,64]{1,0:T(8,128)S(1)} %get-tuple-element.63), kind=kOutput, calls=%fused_computation.8 | convolution fusion | flops 274731008 | bytes 8536320 | tf_op jit(solution)/shard_map/dot_general | solution.py:111
  209.6 5.5 %fusion.3 = bf16[64,32768]{1,0:T(8,128)(2,1)} fusion(bf16[64,32768]{1,0:T(8,128)(2,1)} %bitcast.29, f32[64]{0:T(128)S(1)} %broadcast_subtract_fusion, f32[32768]{0:T(1024)S(1)} %broadcast_multiply_fusion.1, f32[64,64]{1,0:T(8,128)S(1)} %get-tuple-element.63), kind=kOutput, calls=%fused_computation.7 | convolution fusion | flops 274731008 | bytes 8536320 | tf_op jit(solution)/shard_map/dot_general | solution.py:111
  (133 shorter events, 10.0 us)
Async XLA Ops:
  16.6 5.5 %copy-start.3 = (f32[2,256,16]{1,2,0:T(8,128)S(1)}, f32[2,256,16]{1,2,0:T(8,128)}, u32[]{:S(2)}) copy-start(f32[2,256,16]{1,2,0:T(8,128)} %param.12) | copy-start | bytes 98308
  16.7 6.1 %copy-start.2 = (f32[2,256,16]{1,2,0:T(8,128)S(1)}, f32[2,256,16]{1,2,0:T(8,128)}, u32[]{:S(2)}) copy-start(f32[2,256,16]{1,2,0:T(8,128)} %param.13) | copy-start | bytes 98308
  16.7 6.4 %copy-start.4 = (s32[2,256]{1,0:T(2,128)S(1)}, s32[2,256]{1,0:T(2,128)}, u32[]{:S(2)}) copy-start(s32[2,256]{1,0:T(2,128)} %param.11) | copy-start | bytes 6148
  18.6 16.6 %all-to-all-start = ((bf16[2,32,2,4096]{3,1,0,2:T(8,128)(2,1)}), bf16[2,32,2,4096]{3,1,0,2:T(8,128)(2,1)S(1)}, u32[]{:S(2)}, u32[]{:S(2)}) async-start(bf16[2,32,2,4096]{3,1,0,2:T(8,128)(2,1)} %pad_maximum_fusion), calls=%async_computation | async-start | bytes 2097152 | tf_op jit(solution)/shard_map/all_to_all | solution.py:88
  24.1 4.6 %copy-start = (bf16[32,65536]{1,0:T(8,128)(2,1)S(1)}, bf16[32,65536]{1,0:T(8,128)(2,1)}, u32[]{:S(2)}) copy-start(bf16[32,65536]{1,0:T(8,128)(2,1)} %param.8) | copy-start | bytes 12582916
  35.1 117.2 %all-to-all-start.2 = ((bf16[32,2,32768]{2,0,1:T(8,128)(2,1)}), bf16[32,2,32768]{2,0,1:T(8,128)(2,1)}, u32[]{:S(2)}, u32[]{:S(2)}) async-start(bf16[32,2,32768]{2,0,1:T(8,128)(2,1)} %bitcast.124), calls=%async_computation.2 | async-start | bytes 8388608 | tf_op jit(solution)/shard_map/all_to_all | solution.py:99
  152.3 48.9 %all-to-all-start.1 = ((bf16[32,2,32768]{2,0,1:T(8,128)(2,1)}), bf16[32,2,32768]{2,0,1:T(8,128)(2,1)}, u32[]{:S(2)}, u32[]{:S(2)}) async-start(bf16[32,2,32768]{2,0,1:T(8,128)(2,1)} %bitcast.123), calls=%async_computation.1 | async-start | bytes 8388608 | tf_op jit(solution)/shard_map/all_to_all | solution.py:98
  174.1 35.5 %copy-start.1 = (f32[64,64]{1,0:T(8,128)}, f32[64,64]{1,0:T(8,128)S(1)}, u32[]{:S(2)}) copy-start(f32[64,64]{1,0:T(8,128)S(1)} %get-tuple-element.63) | copy-start | bytes 49156
